TPU v7x, 32 devices: a whole 2x2x4 slice. The times are simulated.
32 devices in a mesh: dp: 8 (over y, x, core), tensor: 4 (over z).
Axes of the slice: x: 2, y: 2, z: 4, core: 2. Of those that a mesh axis runs over, the one named last changes fastest.
Arguments:
- teacher_in: bfloat16 [2048, 2048], P('dp'), may hold values from -13 to 13
- teacher_gain: float32 [2, 2048], replicated, may hold values from 0.25 to 1.75
- t_gate: bfloat16 [2, 2048, 5472], P(None, 'dp', 'tensor'), may hold values from -0.125 to 0.125
- t_up: bfloat16 [2, 2048, 5472], P(None, 'dp', 'tensor'), may hold values from -0.125 to 0.125
- t_down: bfloat16 [2, 5472, 2048], P(None, 'tensor', 'dp'), may hold values from -0.078125 to 0.078125
- student_in: bfloat16 [2048, 1024], P('dp'), may hold values from -13 to 13
- student_gain: float32 [2, 1024], replicated, may hold values from 0.3 to 3.5
- s_gate: bfloat16 [2, 1024, 4096], P(None, None, 'tensor'), may hold values from -0.1875 to 0.1875
- s_up: bfloat16 [2, 1024, 4096], P(None, None, 'tensor'), may hold values from -0.1875 to 0.1875
- s_down: bfloat16 [2, 4096, 1024], P(None, 'tensor'), may hold values from -0.09375 to 0.09375
- proj: bfloat16 [1024, 2048], P(None, 'tensor'), may hold values from -1 to 1
- layer_map: int32 [2], replicated, may hold values from 0 to 1, each once
Outputs:
- teacher_states: bfloat16 [2, 2048, 2048], P(None, ('dp', 'tensor'))
- grad_gate: float32 [2, 1024, 4096], P(None, 'dp', 'tensor')
- grad_up: float32 [2, 1024, 4096], P(None, 'dp', 'tensor')
- grad_down: float32 [2, 4096, 1024], P(None, 'tensor', 'dp')
- grad_proj: float32 [1024, 2048], P('dp', 'tensor')
- mean_error: float32 [2], replicated
- grad_rms: float32 [4], replicated
Inputs may be any that keep to these rules, and one draw needn't show every extreme that they name: `layer_map`: each teacher sublayer is matched to exactly one student sublayer.
All inputs are finite; a program needn't handle non-finite values.
Results may differ from a plain program's by a relative error of at most 0.02.
Values may be sent and summed in bfloat16 or wider, within the bound.
No kernel may reach another device: no remote copies, remote signals or barrier semaphores. Data moves between devices by JAX's collectives and lax.ppermute only.
A program may use at most 128 MiB of HBM per device.

v0:
```python
import jax
import jax.numpy as jnp
from jax import lax
from jax.sharding import PartitionSpec as P

DT = 2048
DS = 1024
FS = 4096
T_LAYERS = 2
S_LAYERS = 2
SEQ = 512


EPSILON = 1e-05


def inverse_rms(values):
    return lax.rsqrt(jnp.mean(values * values, axis=-1, keepdims=True) + EPSILON)


def contract_rows(left, right):
    return lax.dot_general(
        left, right, (((0,), (0,)), ((), ())), preferred_element_type=jnp.float32
    )


def contract_cols(left, right):
    return lax.dot_general(
        left, right, (((1,), (1,)), ((), ())), preferred_element_type=jnp.float32
    )


def per_device(
    teacher_in,
    teacher_gain,
    t_gate,
    t_up,
    t_down,
    student_in,
    student_gain,
    s_gate,
    s_up,
    s_down,
    proj,
    layer_map,
):
    tensor_count = lax.axis_size("tensor")
    tensor_pos = lax.axis_index("tensor")
    token_count = teacher_in.shape[0]
    own_rows = token_count // tensor_count
    row_start = tensor_pos * own_rows
    state = teacher_in
    own_states = []
    full_states = []
    for k in range(T_LAYERS):
        state_wide = state.astype(jnp.float32)
        normed = (state_wide * inverse_rms(state_wide) * teacher_gain[k]).astype(jnp.bfloat16)
        gate_act = jnp.dot(
            normed,
            lax.all_gather(t_gate[k], "dp", axis=0, tiled=True),
            preferred_element_type=jnp.float32,
        )
        up_act = jnp.dot(
            normed,
            lax.all_gather(t_up[k], "dp", axis=0, tiled=True),
            preferred_element_type=jnp.float32,
        )
        hidden = (jax.nn.silu(gate_act) * up_act).astype(jnp.bfloat16)
        down_full = lax.all_gather(t_down[k], "dp", axis=1, tiled=True)
        summed = lax.psum(
            jnp.dot(hidden, down_full, preferred_element_type=jnp.float32).astype(jnp.bfloat16),
            "tensor",
        ).astype(jnp.float32)
        state = (state_wide + summed).astype(jnp.bfloat16)
        own_new = lax.dynamic_slice_in_dim(state, row_start, own_rows, 0)
        own_states.append(own_new)
        full_states.append(state)
    col_width = proj.shape[1]
    col_start = tensor_pos * col_width
    targets = jnp.stack(
        [lax.dynamic_slice_in_dim(full, col_start, col_width, 1) for full in full_states]
    )
    states = [student_in]
    normeds, gates, ups, units, scales = ([], [], [], [], [])
    for l in range(S_LAYERS):
        wide = states[l].astype(jnp.float32)
        scale = inverse_rms(wide)
        normed = (wide * scale * student_gain[l]).astype(jnp.bfloat16)
        gate_act = jnp.dot(normed, s_gate[l], preferred_element_type=jnp.float32)
        up_act = jnp.dot(normed, s_up[l], preferred_element_type=jnp.float32)
        units_now = (jax.nn.silu(gate_act) * up_act).astype(jnp.bfloat16)
        down_now = s_down[l]
        student_part = lax.psum_scatter(
            jnp.dot(units_now, down_now, preferred_element_type=jnp.float32).astype(jnp.bfloat16),
            "tensor",
            scatter_dimension=0,
            tiled=True,
        ).astype(jnp.float32)
        own_wide = lax.dynamic_slice_in_dim(wide, row_start, own_rows, 0)
        own_next = (own_wide + student_part).astype(jnp.bfloat16)
        states.append(lax.all_gather(own_next, "tensor", axis=0, tiled=True))
        normeds.append(normed)
        gates.append(gate_act)
        ups.append(up_act)
        units.append(units_now)
        scales.append(scale)
    error_parts = []
    deltas = []
    for l in range(S_LAYERS):
        predicted = jnp.dot(states[l + 1], proj, preferred_element_type=jnp.float32)
        target = lax.dynamic_index_in_dim(targets, layer_map[l], 0, keepdims=False).astype(
            jnp.float32
        )
        errors = predicted - target
        error_parts.append(jnp.sum(errors * errors))
        deltas.append((errors * (2.0 / (S_LAYERS * SEQ))).astype(jnp.bfloat16))
    error_local = jnp.stack(error_parts)
    error_total = lax.psum(error_local, ("dp", "tensor"))
    grad_x = lax.psum(
        contract_cols(deltas[S_LAYERS - 1], proj).astype(jnp.bfloat16), "tensor"
    ).astype(jnp.float32)
    gate_grads = [None] * S_LAYERS
    up_grads = [None] * S_LAYERS
    down_grads = [None] * S_LAYERS
    for l in reversed(range(S_LAYERS)):
        grad_out = grad_x.astype(jnp.bfloat16)
        grad_units = contract_cols(grad_out, s_down[l])
        sigma = jax.nn.sigmoid(gates[l])
        grad_gate_act = (grad_units * ups[l] * sigma * (1.0 + gates[l] * (1.0 - sigma))).astype(
            jnp.bfloat16
        )
        grad_up_act = (grad_units * jax.nn.silu(gates[l])).astype(jnp.bfloat16)
        gate_grads[l] = contract_rows(normeds[l], grad_gate_act)
        up_grads[l] = contract_rows(normeds[l], grad_up_act)
        down_grads[l] = contract_rows(units[l], grad_out)
        if l > 0:
            norm_part = contract_cols(grad_gate_act, s_gate[l]) + contract_cols(
                grad_up_act, s_up[l]
            )
            proj_part = contract_cols(deltas[l - 1], proj)
            grad_norm, grad_side = (
                lax.psum(norm_part.astype(jnp.bfloat16), "tensor").astype(jnp.float32),
                lax.psum(proj_part.astype(jnp.bfloat16), "tensor").astype(jnp.float32),
            )
            wide = states[l].astype(jnp.float32)
            scaled = grad_norm * student_gain[l]
            through = scales[l] * scaled - wide * scales[l] ** 3 * jnp.mean(
                wide * scaled, axis=-1, keepdims=True
            )
            grad_x = grad_x + through + grad_side
    proj_local = contract_rows(states[1], deltas[0])
    l = 1
    proj_local = proj_local + contract_rows(states[l + 1], deltas[l])
    grad_gate, grad_up, grad_down, grad_proj = (
        lax.psum_scatter(
            jnp.stack(gate_grads).astype(jnp.bfloat16), "dp", scatter_dimension=1, tiled=True
        ).astype(jnp.float32),
        lax.psum_scatter(
            jnp.stack(up_grads).astype(jnp.bfloat16), "dp", scatter_dimension=1, tiled=True
        ).astype(jnp.float32),
        lax.psum_scatter(
            jnp.stack(down_grads).astype(jnp.bfloat16), "dp", scatter_dimension=2, tiled=True
        ).astype(jnp.float32),
        lax.psum_scatter(
            proj_local.astype(jnp.bfloat16), "dp", scatter_dimension=0, tiled=True
        ).astype(jnp.float32),
    )
    squares = jnp.stack(
        [
            jnp.sum(grad_gate * grad_gate),
            jnp.sum(grad_up * grad_up),
            jnp.sum(grad_down * grad_down),
            jnp.sum(grad_proj * grad_proj),
        ]
    )
    square_total = lax.psum(squares, ("dp", "tensor"))
    counts = jnp.array(
        [S_LAYERS * DS * FS, S_LAYERS * DS * FS, S_LAYERS * DS * FS, DS * DT], jnp.float32
    )
    mean_error = error_total / (token_count * lax.axis_size("dp") * DT)
    grad_rms = jnp.sqrt(square_total / counts)
    return (jnp.stack(own_states), grad_gate, grad_up, grad_down, grad_proj, mean_error, grad_rms)


def solution(mesh):
    return jax.shard_map(
        per_device,
        mesh=mesh,
        in_specs=(
            P("dp", None),
            P(),
            P(None, "dp", "tensor"),
            P(None, "dp", "tensor"),
            P(None, "tensor", "dp"),
            P("dp", None),
            P(),
            P(None, None, "tensor"),
            P(None, None, "tensor"),
            P(None, "tensor", None),
            P(None, "tensor"),
            P(),
        ),
        out_specs=(
            P(None, ("dp", "tensor"), None),
            P(None, "dp", "tensor"),
            P(None, "dp", "tensor"),
            P(None, "tensor", "dp"),
            P("dp", "tensor"),
            P(),
            P(),
        ),
        check_vma=False,
    )
```

profile of v0, /device:TPU:0, one launch (start us, length us, event | category | flops | bytes accessed | tf_op | source)
XLA Modules:
  0.0 709.8 jit_solution(3058975793029169596)
XLA Ops:
  8.1 2.7 fusion.110
  12.1 2.5 fusion.112
  14.9 2.5 fusion.56
  17.7 1.8 multiply_convert_fusion.6
  21.0 1.5 fusion.71
  23.0 34.2 %all-gather.13.cloned.1.call-done = bf16[1,2048,1368]{1,2,0:T(8,128)(2,1)} async-done(((bf16[1,256,1368]{1,2,0:T(8,128)(2,1)}), bf16[1,2048,1368]{1,2,0:T(8,128)(2,1)}) %all-gather.13.cloned.1.call-update) | async-done | bytes 5603344 | tf_op jit(solution)/shard_map/all_gather | solution.py:60
  57.2 5.5 fusion.10
  62.6 40.5 %all-gather.15.cloned.1.call-done = bf16[1,2048,1368]{1,2,0:T(8,128)(2,1)} async-done(((bf16[1,256,1368]{1,2,0:T(8,128)(2,1)}), bf16[1,2048,1368]{1,2,0:T(8,128)(2,1)}) %all-gather.15.cloned.1.call-update) | async-done | bytes 5603344 | tf_op jit(solution)/shard_map/all_gather | solution.py:65
  103.2 46.0 %all-gather.17.cloned.1.call-done = bf16[1,1368,2048]{2,1,0:T(8,128)(2,1)} async-done(((bf16[1,1368,256]{2,1,0:T(8,128)(2,1)}), bf16[1,1368,2048]{2,1,0:T(8,128)(2,1)}) %all-gather.17.cloned.1.call-update) | async-done | bytes 5603344 | tf_op jit(solution)/shard_map/all_gather | solution.py:69
  149.2 11.8 %fusion.24 = bf16[256,2048]{1,0:T(8,128)(2,1)} fusion(bf16[1,1368,2048]{2,1,0:T(8,128)(2,1)} %all-gather.17.cloned.1.call-done, bf16[1,2048,1368]{1,2,0:T(8,128)(2,1)} %all-gather.15.cloned.1.call-done, f32[256,1368]{0,1:T(8,128)} %fusion.10, bf16[256,2048]{1,0:T(8,128)(2,1)S(1)} %copy-done.3, f32[2048]{0:T(1024)S(1)} %bitcast.152, f32[256]{0:T(256)S(1)} %add_rsqrt_fusion.3), kind=kOutput, calls=%fused_computation.25 | convolution fusion | flops 2873626624 | bytes 14713856 | tf_op jit(solution)/shard_map/dot_general | solution.py:71
  164.0 22.9 %all_gather.30 = bf16[256,1024]{1,0:T(8,128)(2,1)S(1)} all-gather(bf16[64,1024]{1,0:T(8,128)(2,1)S(1)} %add_convert_fusion.3), channel_id=1, replica_groups=mesh['dp'=8,'tensor'=4] {'tensor'}, dimensions={0}, use_global_device_ids=true | all-gather | bytes 655360 | tf_op jit(solution)/shard_map/all_gather | solution.py:101
  187.1 2.6 fusion.48
  190.2 1.8 multiply_convert_fusion.4
  193.4 1.5 fusion.74
  195.0 25.4 %all-reduce.7.cloned.1.call-done = bf16[256,2048]{1,0:T(8,128)(2,1)} async-done(((bf16[256,2048]{1,0:T(8,128)(2,1)}), bf16[256,2048]{1,0:T(8,128)(2,1)}) %all-reduce.7.cloned.1.call-update) | async-done | bytes 1048592 | tf_op jit(solution)/shard_map/psum | solution.py:70
  220.4 2.0 fusion.34
  222.5 5.5 fusion.4
  228.0 24.4 %all-gather.21.cloned.1.call-done = bf16[1,2048,1368]{1,2,0:T(8,128)(2,1)} async-done(((bf16[1,256,1368]{1,2,0:T(8,128)(2,1)}), bf16[1,2048,1368]{1,2,0:T(8,128)(2,1)}) %all-gather.21.cloned.1.call-update) | async-done | bytes 5603344 | tf_op jit(solution)/shard_map/all_gather | solution.py:65
  252.4 45.3 %all-gather.23.cloned.1.call-done = bf16[1,1368,2048]{2,1,0:T(8,128)(2,1)} async-done(((bf16[1,1368,256]{2,1,0:T(8,128)(2,1)}), bf16[1,1368,2048]{2,1,0:T(8,128)(2,1)}) %all-gather.23.cloned.1.call-update) | async-done | bytes 5603344 | tf_op jit(solution)/shard_map/all_gather | solution.py:69
  297.7 11.8 %fusion.27 = bf16[256,2048]{1,0:T(8,128)(2,1)} fusion(bf16[1,1368,2048]{2,1,0:T(8,128)(2,1)} %all-gather.23.cloned.1.call-done, bf16[1,2048,1368]{1,2,0:T(8,128)(2,1)} %all-gather.21.cloned.1.call-done, f32[256,1368]{0,1:T(8,128)} %fusion.4, bf16[256,2048]{1,0:T(8,128)(2,1)S(1)} %get-tuple-element.20, f32[2048]{0:T(1024)S(1)} %bitcast.150, ...), kind=kOutput, calls=%fused_computation.26 | convolution fusion | flops 2873626624 | bytes 14713856 | tf_op jit(solution)/shard_map/dot_general | solution.py:71
  316.2 22.9 %all_gather.31 = bf16[256,1024]{1,0:T(8,128)(2,1)} all-gather(bf16[64,1024]{1,0:T(8,128)(2,1)S(1)} %add_convert_fusion.2), channel_id=1, replica_groups=mesh['dp'=8,'tensor'=4] {'tensor'}, dimensions={0}, use_global_device_ids=true | all-gather | bytes 655360 | tf_op jit(solution)/shard_map/all_gather | solution.py:101
  339.1 30.6 %all-reduce.9.cloned.1.call-done = bf16[256,2048]{1,0:T(8,128)(2,1)} async-done(((bf16[256,2048]{1,0:T(8,128)(2,1)}), bf16[256,2048]{1,0:T(8,128)(2,1)}) %all-reduce.9.cloned.1.call-update) | async-done | bytes 1048592 | tf_op jit(solution)/shard_map/psum | solution.py:70
  369.8 1.7 fusion.37
  376.0 2.1 multiply_reduce_fusion.7
  380.1 33.7 %all-reduce.11.cloned.1.call-done = bf16[256,1024]{1,0:T(8,128)(2,1)} async-done(((bf16[256,1024]{1,0:T(8,128)(2,1)}), bf16[256,1024]{1,0:T(8,128)(2,1)}) %all-reduce.11.cloned.1.call-update) | async-done | bytes 524304 | tf_op jit(solution)/shard_map/psum | solution.py:119
  413.8 3.5 multiply_convert_fusion.2
  419.1 1.5 fusion.77
  421.8 1.5 add_convert_fusion
  423.4 3.1 convert_bitcast_fusion
  426.5 45.5 %all-reduce.13.cloned.1.call-done = (bf16[256,1024]{1,0:T(8,128)(2,1)}, bf16[256,1024]{1,0:T(8,128)(2,1)}) async-done(((bf16[256,1024]{1,0:T(8,128)(2,1)}, bf16[256,1024]{1,0:T(8,128)(2,1)}), (bf16[256,1024]{1,0:T(8,128)(2,1)}, bf16[256,1024]{1,0:T(8,128)(2,1)})) %all-reduce.13.cloned.1.call-update) | async-done | bytes 1048592 | tf_op jit(solution)/shard_map/psum | solution.py:143
  473.4 1.6 add_convert_fusion.1
  476.7 2.3 pad_maximum_fusion.2
  479.0 11.3 %copy.20 = bf16[2,1024,1024]{1,0,2:T(2,128)(2,1)} copy(bf16[2,1024,1024]{2,1,0:T(8,128)(2,1)} %pad_maximum_fusion.2) | data formatting | bytes 8388608
  490.3 5.6 copy.22
  497.8 2.4 fusion.50
  502.1 2.3 pad_maximum_fusion.1
  508.7 2.3 pad_maximum_fusion
  511.1 1.4 pad_maximum_fusion.4
  513.4 2.3 multiply_reduce_fusion.8
  515.7 30.8 %reduce-scatter.19.cloned.1.call-done = bf16[128,2048]{1,0:T(8,128)(2,1)} async-done(((bf16[1024,2048]{1,0:T(8,128)(2,1)}), bf16[128,2048]{1,0:T(8,128)(2,1)}) %reduce-scatter.19.cloned.1.call-update) | async-done | bytes 524304
  546.5 1.4 reshape.69
  548.5 1.8 multiply_reduce_fusion
  550.3 50.8 %reduce-scatter.15.cloned.1.call-done = bf16[2,128,1024]{2,1,0:T(8,128)(2,1)} async-done(((bf16[2,1024,1024]{2,1,0:T(8,128)(2,1)}), bf16[2,128,1024]{2,1,0:T(8,128)(2,1)}) %reduce-scatter.15.cloned.1.call-update) | async-done | bytes 524304 | tf_op jit(solution)/shard_map/reduce_scatter | solution.py:158
  601.0 2.8 multiply_reduce_fusion.1
  603.8 51.5 %reduce-scatter.13.cloned.1.call-done = bf16[2,128,1024]{2,1,0:T(8,128)(2,1)} async-done(((bf16[2,1024,1024]{2,1,0:T(8,128)(2,1)}), bf16[2,128,1024]{2,1,0:T(8,128)(2,1)}) %reduce-scatter.13.cloned.1.call-update) | async-done | bytes 524304 | tf_op jit(solution)/shard_map/reduce_scatter | solution.py:155
  655.4 2.8 multiply_reduce_fusion.2
  658.2 2.6 pad_maximum_fusion.5
  661.7 39.2 %all-reduce = (f32[2]{0:T(128)S(1)}, f32[4]{0:T(128)S(1)}) all-reduce(f32[2]{0:T(128)S(1)} %pad_maximum_fusion.4, f32[4]{0:T(128)S(1)} %pad_maximum_fusion.5), channel_id=1, replica_groups=mesh['dp'=8,'tensor'=4] {'dp','tensor'}, use_global_device_ids=true, to_apply=%region_18.19 | all-reduce | flops 6 | bytes 48 | tf_op jit(solution)/shard_map/psum | solution.py:118
  (149 shorter events, 35.5 us)
Async XLA Ops:
  8.0 364.5 %copy-start = (bf16[1024,512]{1,0:T(8,128)(2,1)S(1)}, bf16[1024,512]{1,0:T(8,128)(2,1)}, u32[]{:S(2)}) copy-start(bf16[1024,512]{1,0:T(8,128)(2,1)} %param.23) | copy-start | bytes 3145732
  8.0 2.8 copy-start.13
  8.0 49.1 %all-gather.13.cloned.1.call-start = ((), (), s32[]{:S(2)}) async-start(), calls=%async_computation.14 | async-start | bytes 6303744 | tf_op jit(solution)/shard_map/all_gather | solution.py:60
  10.7 92.4 %all-gather.15.cloned.1.call-start = ((), (), s32[]{:S(2)}) async-start(), calls=%async_computation.15 | async-start | bytes 6303744 | tf_op jit(solution)/shard_map/all_gather | solution.py:65
  12.0 2.7 copy-start.5
  12.0 2.9 copy-start.23
  12.0 137.2 %all-gather.17.cloned.1.call-start = ((), (), s32[]{:S(2)}) async-start(), calls=%async_computation.16 | async-start | bytes 6303744 | tf_op jit(solution)/shard_map/all_gather | solution.py:69
  14.6 148.4 %reduce-scatter.9.cloned.1.call-start = ((), (), s32[]{:S(2)}) async-start(), calls=%async_computation.8 | async-start | bytes 655360 | tf_op jit(solution)/shard_map/reduce_scatter | solution.py:93
  14.9 2.8 copy-start.25
  17.7 1.8 copy-start.34
  17.7 3.3 copy-start.29
  21.0 1.6 copy-start.22
  21.0 1.6 copy-start.3
  22.6 197.9 %all-reduce.7.cloned.1.call-start = ((), (), s32[]{:S(2)}) async-start(), calls=%async_computation.6 | async-start | bytes 2097152 | tf_op jit(solution)/shard_map/psum | solution.py:70
  161.1 61.4 %all-gather.19.cloned.1.call-start = ((), (), s32[]{:S(2)}) async-start(), calls=%async_computation.17 | async-start | bytes 6303744 | tf_op jit(solution)/shard_map/all_gather | solution.py:60
  161.7 90.7 %all-gather.21.cloned.1.call-start = ((), (), s32[]{:S(2)}) async-start(), calls=%async_computation.18 | async-start | bytes 6303744 | tf_op jit(solution)/shard_map/all_gather | solution.py:65
  162.2 135.4 %all-gather.23.cloned.1.call-start = ((), (), s32[]{:S(2)}) async-start(), calls=%async_computation.19 | async-start | bytes 6303744 | tf_op jit(solution)/shard_map/all_gather | solution.py:69
  162.8 152.3 %reduce-scatter.11.cloned.1.call-start = ((), (), s32[]{:S(2)}) async-start(), calls=%async_computation.9 | async-start | bytes 655360 | tf_op jit(solution)/shard_map/reduce_scatter | solution.py:93
  187.1 3.2 copy-start.26
  190.2 1.9 copy-start.37
  190.2 3.2 copy-start.30
  194.9 174.9 %all-reduce.9.cloned.1.call-start = ((), (), s32[]{:S(2)}) async-start(), calls=%async_computation.7 | async-start | bytes 2097152 | tf_op jit(solution)/shard_map/psum | solution.py:70
  228.0 81.6 %copy-start.24 = (s32[2]{0:T(128)S(1)}, s32[2]{0:T(128)}, u32[]{:S(2)}) copy-start(s32[2]{0:T(128)} %param.24) | copy-start | bytes 28
  309.5 104.3 %all-reduce.11.cloned.1.call-start = ((), (), s32[]{:S(2)}) async-start(), calls=%async_computation.10 | async-start | bytes 1048576 | tf_op jit(solution)/shard_map/psum | solution.py:119
  369.8 2.7 copy-start.9
  372.5 1.1 copy-start.21
  375.7 96.3 %all-reduce.13.cloned.1.call-start = ((), (), s32[]{:S(2)}) async-start(), calls=%async_computation.21 | async-start | bytes 2097152 | tf_op jit(solution)/shard_map/psum | solution.py:143
  413.8 3.6 copy-start.27
  413.8 5.3 copy-start.28
  417.3 3.3 copy-start.17
  419.1 1.6 copy-start.8
  420.6 1.0 copy-start.10
  420.6 92.8 %reduce-scatter.17.cloned.1.call-start = ((), (), s32[]{:S(2)}) async-start(), calls=%async_computation.13 | async-start | bytes 1179648 | tf_op jit(solution)/shard_map/reduce_scatter | solution.py:164
  420.7 1.1 copy-start.12
  421.8 1.5 copy-start.6
  423.3 123.2 %reduce-scatter.19.cloned.1.call-start = ((), (), s32[]{:S(2)}) async-start(), calls=%async_computation.20 | async-start | bytes 4718592
  472.1 3.0 copy-start.15
  475.1 1.6 copy-start.2
  495.9 1.0 copy-start.20
  495.9 105.1 %reduce-scatter.15.cloned.1.call-start = ((), (), s32[]{:S(2)}) async-start(), calls=%async_computation.12 | async-start | bytes 4718592 | tf_op jit(solution)/shard_map/reduce_scatter | solution.py:158
  497.8 3.4 copy-start.35
  504.4 1.1 copy-start.18
  504.5 150.9 %reduce-scatter.13.cloned.1.call-start = ((), (), s32[]{:S(2)}) async-start(), calls=%async_computation.11 | async-start | bytes 4718592 | tf_op jit(solution)/shard_map/reduce_scatter | solution.py:155
  505.5 1.3 copy-start.33
  505.5 1.8 copy-start.36
  505.5 2.2 copy-start.38
  548.5 153.5 %copy-start.1 = (bf16[1024,512]{1,0:T(8,128)(2,1)S(1)}, bf16[1024,512]{1,0:T(8,128)(2,1)}, u32[]{:S(2)}) copy-start(bf16[1024,512]{1,0:T(8,128)(2,1)} %param.23) | copy-start | bytes 3145732
  550.3 151.2 %copy-start.31 = (f32[4]{0:T(128)S(1)}, f32[4]{0:T(128)}, u32[]{:S(2)}) copy-start(f32[4]{0:T(128)} %constant.52) | copy-start | bytes 52
  (7 other events, 6.0 us)
Sparse Core Ops, SparseCore 0:
  10.9 46.2 all-gather.12
  59.6 43.5 all-gather.14
  105.7 43.5 all-gather.16
  163.5 43.5 all-gather.18
  208.8 43.5 all-gather.20
  254.1 43.5 all-gather.22
  424.6 35.5 reduce-scatter.16
  496.0 50.4 reduce-scatter.18
  549.9 51.0 reduce-scatter.14
  604.2 51.0 reduce-scatter.12
Sparse Core Ops, SparseCore 1:
  22.7 24.5 reduce-scatter.8
  161.2 59.2 all-reduce.6
  223.2 21.0 reduce-scatter.10
  309.6 60.1 all-reduce.8
  375.8 38.0 all-reduce.10
  420.7 51.3 all-reduce.12
where the time goes:
time: 718 us; the launch traced here: 710 us
  waiting for transfers between devices  461 us (64%)
  blocking collectives  85 us (12%)
  matrix products  69.7 us (10%)
  local copies, waits for them, and re-layouts  39.6 us (6%)
  other arithmetic  33.1 us (5%)
  between operations  20.5 us (3%)
    all_gather x2, waiting for transfers between devices, per_device(): down_full = lax.all_gather(t_down[k], 'dp', axis=1, tiled=True)  91.3 us
    all_gather x2, waiting for transfers between devices, per_device(): lax.all_gather(t_up[k], 'dp', axis=0, tiled=True)  64.9 us
    psum x2, waiting for transfers between devices, per_device(): lax.psum(jnp.dot(hidden, down_full, preferred_element_type=jnp.float32).a...  56.1 us
    reduce_scatter x1, waiting for transfers between devices, per_device(): lax.psum_scatter(jnp.stack(gate_grads).astype(jnp.bfloat16), 'dp', scatte...  51.5 us
    reduce_scatter x1, waiting for transfers between devices, per_device(): lax.psum_scatter(jnp.stack(up_grads).astype(jnp.bfloat16), 'dp', scatter_...  50.8 us
    all_gather x2, blocking collectives, per_device(): states.append(lax.all_gather(own_next, 'tensor', axis=0, tiled=True))  45.8 us
    psum x1, waiting for transfers between devices, per_device(): lax.psum(proj_part.astype(jnp.bfloat16), 'tensor').astype(jnp.float32)  45.5 us
    psum x1, blocking collectives, per_device(): error_total = lax.psum(error_local, ('dp', 'tensor'))  39.2 us
  transfers between devices with their start and end apart: 16, of which 12 were waited for; matrix products, arithmetic and copies ran while one was open for 15% of the time, Pallas kernels for 0%

commit v1 on v0

v1 whole, which is shorter than its diff:
```python
import jax
import jax.numpy as jnp
from jax import lax
from jax.sharding import Mesh
from jax.sharding import PartitionSpec as P

SEQ = 512
EPSILON = 1e-05
F32 = jnp.float32
BF16 = jnp.bfloat16
CHIP = ("row", "col")


def inverse_rms(values):
    return lax.rsqrt(jnp.mean(values * values, axis=-1, keepdims=True) + EPSILON)


def dot(left, right):
    return jnp.dot(left, right, preferred_element_type=F32)


def contract_rows(left, right):
    return lax.dot_general(left, right, (((0,), (0,)), ((), ())), preferred_element_type=F32)


def contract_cols(left, right):
    return lax.dot_general(left, right, (((1,), (1,)), ((), ())), preferred_element_type=F32)


def pull(value, axis, shift):
    n = lax.axis_size(axis)
    return lax.ppermute(value, axis, [(j, (j - shift) % n) for j in range(n)])


def push(value, axis, shift):
    n = lax.axis_size(axis)
    return lax.ppermute(value, axis, [(j, (j + shift) % n) for j in range(n)])


def swap(value):
    return lax.ppermute(value, "core", [(0, 1), (1, 0)])


def chip_shifts():
    return [(r, c) for r in range(lax.axis_size("row")) for c in range(lax.axis_size("col"))]


def push_chip(value, shift):
    rows, cols = lax.axis_size("row"), lax.axis_size("col")
    pairs = [
        (r * cols + c, ((r + shift[0]) % rows) * cols + (c + shift[1]) % cols)
        for r in range(rows)
        for c in range(cols)
    ]
    return lax.ppermute(value, CHIP, pairs)


def chip_index(shift):
    rows, cols = lax.axis_size("row"), lax.axis_size("col")
    row = lax.rem(lax.axis_index("row") + shift[0], rows)
    col = lax.rem(lax.axis_index("col") + shift[1], cols)
    return row * cols + col


def gather_chips(block, axis):
    half = block.shape[axis] // 2
    rows, cols = lax.axis_size("row"), lax.axis_size("col")
    found = {(0, 0): block}
    for c in range(1, cols):
        found[(0, c)] = pull(block, "col", c)
    for r in range(1, rows):
        found[(r, 0)] = pull(block, "row", r)
    for r in range(1, rows):
        for c in range(1, cols):
            first = lax.slice_in_dim(found[(0, c)], 0, half, axis=axis)
            last = lax.slice_in_dim(found[(r, 0)], half, None, axis=axis)
            found[(r, c)] = jnp.concatenate(
                [pull(first, "row", r), pull(last, "col", c)], axis=axis
            )
    return [found[s] for s in chip_shifts()]


def take_blocks(value, axis, width, starts):
    return jnp.concatenate(
        [lax.dynamic_slice_in_dim(value, s * width, width, axis) for s in starts], axis=axis
    )


def per_device(
    teacher_in,
    teacher_gain,
    t_gate,
    t_up,
    t_down,
    student_in,
    student_gain,
    s_gate,
    s_up,
    s_down,
    proj,
    layer_map,
):
    n = lax.axis_size("tensor")
    pos = lax.axis_index("tensor")
    core = lax.axis_index("core")
    shifts = chip_shifts()
    chips = len(shifts)
    t_layers = t_gate.shape[0]
    s_layers = s_gate.shape[0]
    tokens, dt = teacher_in.shape
    ds = student_in.shape[1]
    own = tokens // n
    share = dt // (2 * chips)
    positions = [lax.rem(pos + k, n) for k in range(n)]
    groups = [chip_index(s) for s in shifts]
    mine_cols = [g * 2 + core for g in groups]
    other_cols = [g * 2 + 1 - core for g in groups]

    def sum_rows(part):
        total = part[:own].astype(F32)
        for k in range(1, n):
            total = total + push(part[k * own : (k + 1) * own], "tensor", k).astype(F32)
        return total

    def gather_rows(rows):
        return jnp.concatenate([rows] + [pull(rows, "tensor", k) for k in range(1, n)])

    weights = []
    for k in range(t_layers):
        weights.append(
            (
                gather_chips(t_gate[k], 0),
                gather_chips(t_up[k], 0),
                gather_chips(t_down[k], 1),
            )
        )

    x = take_blocks(student_in, 0, own, positions)
    states, x_rows = [x], [x[:own].astype(F32)]
    normeds, gates, ups, units, scales = [], [], [], [], []
    for l in range(s_layers):
        wide = states[l].astype(F32)
        scale = inverse_rms(wide)
        normed = (wide * scale * student_gain[l]).astype(BF16)
        gate_act = dot(normed, s_gate[l])
        up_act = dot(normed, s_up[l])
        unit = (jax.nn.silu(gate_act) * up_act).astype(BF16)
        part = dot(unit, s_down[l]).astype(BF16)
        next_rows = (x_rows[l] + sum_rows(part)).astype(BF16)
        x_rows.append(next_rows.astype(F32))
        states.append(gather_rows(next_rows))
        normeds.append(normed)
        gates.append(gate_act)
        ups.append(up_act)
        units.append(unit)
        scales.append(scale)

    proj_mine = lax.dynamic_slice_in_dim(proj, core * share, share, 1)
    proj_cols = jnp.concatenate(
        [proj_mine] + [pull(proj_mine, "tensor", k) for k in range(1, n)], axis=1
    )
    predicted = []
    for l in range(s_layers):
        rows = x_rows[l + 1].astype(BF16)
        predicted.append(dot(jnp.concatenate([rows, swap(rows)]), proj_cols))

    wide = teacher_in.astype(F32)
    normed = (wide * inverse_rms(wide) * teacher_gain[0]).astype(BF16)
    normed = take_blocks(normed, 0, own, positions)
    kept = take_blocks(normed, 1, share, mine_cols)
    given = take_blocks(normed, 1, share, other_cols)
    normed = jnp.concatenate([kept, swap(given)])
    rows = lax.dynamic_slice_in_dim(teacher_in, pos * own, own, 0)
    state = jnp.concatenate(
        [take_blocks(rows, 1, share, mine_cols), swap(take_blocks(rows, 1, share, other_cols))]
    ).astype(F32)
    gain_mine = take_blocks(teacher_gain, 1, share, mine_cols)
    home = [lax.axis_index("row"), lax.axis_index("col")]

    def to_plain(value, first):
        rows_n, cols_n = lax.axis_size("row"), lax.axis_size("col")
        picked = []
        for k in range(chips):
            chip = lax.rem(first + k, chips)
            r = lax.rem(chip // cols_n - home[0] + rows_n, rows_n)
            c = lax.rem(lax.rem(chip, cols_n) - home[1] + cols_n, cols_n)
            picked.append(r * cols_n + c)
        return take_blocks(value, 1, share, picked)

    out_states, targets = [], []
    for k in range(t_layers):
        w_gate, w_up, w_down = weights[k]
        acts = []
        for w in (w_gate, w_up):
            total = dot(normed[:, :share], w[0])
            for i in range(1, chips):
                total = total + dot(normed[:, i * share : (i + 1) * share], w[i])
            acts.append(total[:tokens] + swap(total[tokens:]))
        hidden = (jax.nn.silu(acts[0]) * acts[1]).astype(BF16)
        both = jnp.concatenate([hidden, swap(hidden)])
        part = jnp.concatenate([dot(both, w).astype(BF16) for w in w_down], axis=1)

        def rows_of(j):
            return jnp.concatenate(
                [part[j * own : (j + 1) * own], part[tokens + j * own : tokens + (j + 1) * own]]
            )

        total = rows_of(0).astype(F32)
        for j in range(1, n):
            total = total + push(rows_of(j), "tensor", j).astype(F32)
        narrow = (state + total).astype(BF16)
        state = narrow.astype(F32)
        if k + 1 < t_layers:
            squares = jnp.sum(state * state, axis=-1, keepdims=True)
            across = swap(jnp.concatenate([squares[own:], squares[:own]]))
            inv = lax.rsqrt((squares + across) / dt + EPSILON)
            block = (state * inv * gain_mine[k + 1]).astype(BF16)
            blocks = [block] + [pull(block, "tensor", j) for j in range(1, n)]
            normed = jnp.concatenate([b[:own] for b in blocks] + [b[own:] for b in blocks])
        targets.append(to_plain(narrow, pos))
        mine = to_plain(narrow[:own], 0)
        theirs = swap(to_plain(narrow[own:], 0))
        lower = jnp.where(core == 0, mine, theirs)
        upper = jnp.where(core == 0, theirs, mine)
        pieces = []
        for j in range(chips):
            pieces.append(lower[:, j * share : (j + 1) * share])
            pieces.append(upper[:, j * share : (j + 1) * share])
        out_states.append(jnp.concatenate(pieces, axis=1))
    targets = jnp.stack(targets)

    error_parts, deltas, c_rows = [], [], []
    for l in range(s_layers):
        target = lax.dynamic_index_in_dim(targets, layer_map[l], 0, keepdims=False)
        errors = predicted[l] - target.astype(F32)
        error_parts.append(jnp.sum(errors * errors))
        deltas.append((errors * (2.0 / (s_layers * SEQ))).astype(BF16))
    for l in range(s_layers):
        part = contract_cols(deltas[l], proj_cols)
        c_rows.append(part[:own] + swap(part[own:]))

    ds_mine = [g * 2 + core for g in groups]
    ds_other = [g * 2 + 1 - core for g in groups]
    slot = ds // (2 * chips)

    def by_owner(value):
        return take_blocks(value, 1, slot, ds_mine + ds_other)

    def reduce_blocks(blocks):
        total = blocks[0]
        for s, b in zip(shifts[1:], blocks[1:]):
            total = total + push_chip(b.astype(BF16), s).astype(F32)
        return total

    gate_grads = [None] * s_layers
    up_grads = [None] * s_layers
    down_grads = [None] * s_layers
    grad_rows = c_rows[s_layers - 1]
    for l in reversed(range(s_layers)):
        grad_out = gather_rows(grad_rows.astype(BF16))
        grad_units = contract_cols(grad_out, s_down[l])
        sigma = jax.nn.sigmoid(gates[l])
        grad_gate_act = (
            grad_units * ups[l] * sigma * (1.0 + gates[l] * (1.0 - sigma))
        ).astype(BF16)
        grad_up_act = (grad_units * jax.nn.silu(gates[l])).astype(BF16)
        if l > 0:
            norm_part = contract_cols(grad_gate_act, s_gate[l]) + contract_cols(
                grad_up_act, s_up[l]
            )
            grad_norm = sum_rows(norm_part.astype(BF16))
            wide = x_rows[l]
            scale = scales[l][:own]
            scaled = grad_norm * student_gain[l]
            through = scale * scaled - wide * scale**3 * jnp.mean(
                wide * scaled, axis=-1, keepdims=True
            )
            grad_rows = grad_rows + through + c_rows[l - 1]
        down = contract_rows(units[l], by_owner(grad_out)).astype(BF16)
        half = ds // 2
        down = down[:, :half].astype(F32) + swap(down[:, half:]).astype(F32)
        down_grads[l] = reduce_blocks([down[:, i * slot : (i + 1) * slot] for i in range(chips)])
        acts = jnp.concatenate([grad_gate_act, grad_up_act], axis=1)
        both = contract_rows(by_owner(normeds[l]), acts).astype(BF16)
        both = both[:half].astype(F32) + swap(both[half:]).astype(F32)
        both = reduce_blocks([both[i * slot : (i + 1) * slot] for i in range(chips)])
        width = grad_gate_act.shape[1]
        gate_grads[l] = both[:, :width]
        up_grads[l] = both[:, width:]

    lefts, rights = [], []
    for l in range(s_layers):
        found = [deltas[l][:, :share]]
        for k in range(1, n):
            found.append(push(deltas[l][:, k * share : (k + 1) * share], "tensor", k))
        ordered = [found[(n - k) % n] for k in range(n)]
        rights += [b[:own] for b in ordered] + [b[own:] for b in ordered]
        pair = [states[l + 1], swap(states[l + 1])]
        lefts += [take_blocks(s, 1, 2 * slot, groups) for s in pair]
    wide = contract_rows(jnp.concatenate(lefts), jnp.concatenate(rights))
    wide = reduce_blocks([wide[i * 2 * slot : (i + 1) * 2 * slot] for i in range(chips)])
    kept = jnp.where(core == 0, wide[:slot], wide[slot:])
    given = jnp.where(core == 0, wide[slot:], wide[:slot])
    other = swap(given)
    grad_proj = jnp.concatenate(
        [jnp.where(core == 0, kept, other), jnp.where(core == 0, other, kept)], axis=1
    )

    grad_gate, grad_up, grad_down = jnp.stack(gate_grads), jnp.stack(up_grads), jnp.stack(down_grads)
    sums = jnp.stack(
        error_parts + [jnp.sum(g * g) for g in (grad_gate, grad_up, grad_down, grad_proj)]
    )
    sums = sums + swap(sums)
    got = sums
    for s in shifts[1:]:
        got = got + push_chip(sums, s)
    sums = got
    for k in range(1, n):
        got = got + push(sums, "tensor", k)
    groups_n = 2 * chips
    mean_error = got[:s_layers] / (tokens * groups_n * dt)
    entries = s_layers * ds * s_gate.shape[2] * n
    counts = jnp.array([entries, entries, entries, ds * dt], F32)
    grad_rms = jnp.sqrt(got[s_layers:] / counts)
    return (jnp.stack(out_states), grad_gate, grad_up, grad_down, grad_proj, mean_error, grad_rms)


def solution(mesh):
    dp, n = mesh.shape["dp"], mesh.shape["tensor"]
    view = Mesh(mesh.devices.reshape(dp // 4, 2, 2, n), ("row", "col", "core", "tensor"))
    every = ("row", "col", "core")
    return jax.shard_map(
        per_device,
        mesh=view,
        in_specs=(
            P(every, None),
            P(),
            P(None, every, "tensor"),
            P(None, every, "tensor"),
            P(None, "tensor", every),
            P(every, None),
            P(),
            P(None, None, "tensor"),
            P(None, None, "tensor"),
            P(None, "tensor", None),
            P(None, "tensor"),
            P(),
        ),
        out_specs=(
            P(None, (*every, "tensor"), None),
            P(None, every, "tensor"),
            P(None, every, "tensor"),
            P(None, "tensor", every),
            P(every, "tensor"),
            P(),
            P(),
        ),
        check_vma=False,
    )
```

time: 718 us -> 516 us (0.72)
  waiting for transfers between devices: 461 us -> 246 us
  starting transfers between devices: 1.13 us -> 109 us
  blocking collectives: 85 us -> 0 us
  local copies, waits for them, and re-layouts: 39.6 us -> 64.4 us
  matrix products: 69.7 us -> 52.7 us
  between operations: 20.5 us -> 7.3 us
    ppermute x0 -> x107, waiting for transfers between devices: none -> 246 us  [the longest x42 94.3 us: pull(): return lax.ppermute(value, axis, [(j, (j - shift) % n) for j in range(n)])]
    all_gather x6 -> x0, waiting for transfers between devices: 190 us -> none  [the longest x2 91.3 us: per_device(): down_full = lax.all_gather(t_down[k], 'dp', axis=1, tiled=True)]
    psum x4 -> x0, waiting for transfers between devices: 135 us -> none  [the longest x2 56.1 us: per_device(): lax.psum(jnp.dot(hidden, down_full, preferred_element_type=jnp.float32).a...]
    ppermute x0 -> x107, starting transfers between devices: none -> 109 us  [the longest x42 54.8 us: pull(): return lax.ppermute(value, axis, [(j, (j - shift) % n) for j in range(n)])]
    reduce_scatter x5 -> x0, waiting for transfers between devices: 102 us -> none  [the longest x1 51.5 us: per_device(): lax.psum_scatter(jnp.stack(gate_grads).astype(jnp.bfloat16), 'dp', scatte...]
    all_gather x2 -> x0, blocking collectives: 45.8 us -> none  [per_device(): states.append(lax.all_gather(own_next, 'tensor', axis=0, tiled=True))]
    psum x1 -> x0, blocking collectives: 39.2 us -> none  [per_device(): error_total = lax.psum(error_local, ('dp', 'tensor'))]
    unnamed x17 -> x0, waiting for transfers between devices: 32.6 us -> none
  transfers between devices with their start and end apart: 16 -> 107, of which waited for: 12 -> 56; matrix products, arithmetic and copies ran while one was open for 15% -> 24% of each run, Pallas kernels for 0% -> 0%
where the time goes in v1:
time: 516 us; the launch traced here: 507 us
  waiting for transfers between devices  246 us (48%)
  starting transfers between devices  109 us (21%)
  local copies, waits for them, and re-layouts  64.4 us (12%)
  matrix products  52.7 us (10%)
  other arithmetic  28.3 us (5%)
  between operations  7.3 us (1%)
    ppermute x42, waiting for transfers between devices, pull(): return lax.ppermute(value, axis, [(j, (j - shift) % n) for j in range(n)])  94.3 us
    ppermute x24, waiting for transfers between devices, push(): return lax.ppermute(value, axis, [(j, (j + shift) % n) for j in range(n)])  86.9 us
    ppermute x18, waiting for transfers between devices, push_chip(): return lax.ppermute(value, CHIP, pairs)  63.1 us
    ppermute x42, starting transfers between devices, pull(): return lax.ppermute(value, axis, [(j, (j - shift) % n) for j in range(n)])  54.8 us
    dot_general x32, matrix products, dot(): return jnp.dot(left, right, preferred_element_type=F32)  33.9 us
    ppermute x24, starting transfers between devices, push(): return lax.ppermute(value, axis, [(j, (j + shift) % n) for j in range(n)])  29.5 us
    ppermute x18, starting transfers between devices, push_chip(): return lax.ppermute(value, CHIP, pairs)  20.9 us
    unnamed x209, local copies, waits for them, and re-layouts  17.8 us
  transfers between devices with their start and end apart: 107, of which 56 were waited for; matrix products, arithmetic and copies ran while one was open for 24% of the time, Pallas kernels for 0%

profile of v1, /device:TPU:0, one launch (start us, length us, event | category | flops | bytes accessed | tf_op | source)
XLA Modules:
  0.0 507.4 jit_solution(17747205904938749337)
XLA Ops:
  0.7 2.6 slice_bitcast_fusion.1
  3.3 3.0 collective-permute-start.8
  17.1 3.8 multiply_convert_fusion.5
  25.4 4.0 collective-permute-start.46
  51.5 3.5 collective-permute-done.5
  82.8 2.8 fusion.76
  88.8 6.4 %collective-permute-done.14 = bf16[1368,256]{1,0:T(8,128)(2,1)S(1)} collective-permute-done((bf16[1368,256]{1,0:T(8,128)(2,1)}, bf16[1368,256]{1,0:T(8,128)(2,1)S(1)}, u32[]{:S(2)}, u32[]{:S(2)}) %collective-permute-start.14) | collective-permute-done | bytes 700448 | tf_op jit(solution)/shard_map/ppermute | solution.py:32
  100.2 3.8 collective-permute-done.16
  104.0 12.4 %collective-permute-done.15 = bf16[1368,128]{1,0:T(8,128)(2,1)S(1)} collective-permute-done((bf16[1368,128]{1,0:T(8,128)(2,1)S(1)}, bf16[1368,128]{1,0:T(8,128)(2,1)S(1)}, u32[]{:S(2)}, u32[]{:S(2)}) %collective-permute-start.15) | collective-permute-done | bytes 350240 | tf_op jit(solution)/shard_map/ppermute | solution.py:32
  123.7 2.6 collective-permute-done.19
  126.8 14.4 %collective-permute-done.18 = bf16[128,1024]{0,1:T(8,128)(2,1)S(1)} collective-permute-done((bf16[128,1024]{0,1:T(8,128)(2,1)S(1)}, bf16[128,1024]{0,1:T(8,128)(2,1)S(1)}, u32[]{:S(2)}, u32[]{:S(2)}) %collective-permute-start.18) | collective-permute-done | bytes 262176 | tf_op jit(solution)/shard_map/ppermute | solution.py:37
  144.1 3.1 collective-permute-start.52
  150.8 4.9 collective-permute-done.25
  159.3 20.5 %collective-permute-done.23 = bf16[128,1024]{0,1:T(8,128)(2,1)S(1)} collective-permute-done((bf16[128,1024]{0,1:T(8,128)(2,1)S(1)}, bf16[128,1024]{0,1:T(8,128)(2,1)S(1)}, u32[]{:S(2)}, u32[]{:S(2)}) %collective-permute-start.23) | collective-permute-done | bytes 262176 | tf_op jit(solution)/shard_map/ppermute | solution.py:32
  183.7 2.7 concatenate.192
  205.4 2.8 collective-permute-start.86
  213.1 2.8 collective-permute-done.87
  219.6 7.2 %collective-permute-done.37 = bf16[1368,256]{1,0:T(8,128)(2,1)S(1)} collective-permute-done((bf16[1368,256]{1,0:T(8,128)(2,1)S(1)}, bf16[1368,256]{1,0:T(8,128)(2,1)S(1)}, u32[]{:S(2)}, u32[]{:S(2)}) %collective-permute-start.37) | collective-permute-done | bytes 700448 | tf_op jit(solution)/shard_map/ppermute | solution.py:32
  226.8 5.3 %collective-permute-done.36 = bf16[1368,256]{1,0:T(8,128)(2,1)S(1)} collective-permute-done((bf16[1368,256]{1,0:T(8,128)(2,1)S(1)}, bf16[1368,256]{1,0:T(8,128)(2,1)S(1)}, u32[]{:S(2)}, u32[]{:S(2)}) %collective-permute-start.36) | collective-permute-done | bytes 700448 | tf_op jit(solution)/shard_map/ppermute | solution.py:32
  244.0 4.6 collective-permute-start.42
  251.6 4.2 collective-permute-done.42
  255.8 4.1 collective-permute-start.54
  259.9 24.5 %collective-permute-done.41 = bf16[128,1024]{0,1:T(8,128)(2,1)S(1)} collective-permute-done((bf16[128,1024]{0,1:T(8,128)(2,1)S(1)}, bf16[128,1024]{0,1:T(8,128)(2,1)S(1)}, u32[]{:S(2)}, u32[]{:S(2)}) %collective-permute-start.41) | collective-permute-done | bytes 262176 | tf_op jit(solution)/shard_map/ppermute | solution.py:37
  285.7 9.7 %collective-permute-done.54 = bf16[1024,256]{1,0:T(8,128)(2,1)S(1)} collective-permute-done((bf16[1024,256]{1,0:T(8,128)(2,1)S(1)}, bf16[1024,256]{1,0:T(8,128)(2,1)S(1)}, u32[]{:S(2)}, u32[]{:S(2)}) %collective-permute-start.54) | collective-permute-done | bytes 524320 | tf_op jit(solution)/shard_map/ppermute | solution.py:32
  303.6 3.6 collective-permute-done.90
  307.2 5.8 %collective-permute-done.91 = bf16[128,256]{0,1:T(8,128)(2,1)S(1)} collective-permute-done((bf16[128,256]{0,1:T(8,128)(2,1)S(1)}, bf16[128,256]{0,1:T(8,128)(2,1)S(1)}, u32[]{:S(2)}, u32[]{:S(2)}) %collective-permute-start.91) | collective-permute-done | bytes 65568 | tf_op jit(solution)/shard_map/ppermute | solution.py:37
  313.1 6.1 %collective-permute-done.92 = bf16[128,256]{0,1:T(8,128)(2,1)S(1)} collective-permute-done((bf16[128,256]{0,1:T(8,128)(2,1)S(1)}, bf16[128,256]{0,1:T(8,128)(2,1)S(1)}, u32[]{:S(2)}, u32[]{:S(2)}) %collective-permute-start.92) | collective-permute-done | bytes 65568 | tf_op jit(solution)/shard_map/ppermute | solution.py:37
  319.3 4.9 collective-permute-done.93
  324.8 4.9 collective-permute-done.94
  330.5 5.3 %collective-permute-done.95 = bf16[128,256]{0,1:T(8,128)(2,1)S(1)} collective-permute-done((bf16[128,256]{0,1:T(8,128)(2,1)S(1)}, bf16[128,256]{0,1:T(8,128)(2,1)S(1)}, u32[]{:S(2)}, u32[]{:S(2)}) %collective-permute-start.95) | collective-permute-done | bytes 65568 | tf_op jit(solution)/shard_map/ppermute | solution.py:37
  337.8 6.9 %fusion.232 = (bf16[1024,256]{0,1:T(8,128)(2,1)S(1)}, f32[1024,256]{0,1:T(8,128)}) fusion(bf16[1024,256]{0,1:T(8,128)(2,1)S(1)} %concatenate.226, bf16[256,256]{1,0:T(8,128)(2,1)} %get-tuple-element.114, bf16[256,256]{1,0:T(8,128)(2,1)} %get-tuple-element.115, bf16[256,256]{1,0:T(8,128)(2,1)} %get-tuple-element.116, ...), kind=kOutput, calls=%fused_computation.467 | convolution fusion | flops 570687488 | bytes 4194304 | tf_op jit(solution)/shard_map/dot_general | solution.py:23
  356.0 3.6 collective-permute-start.58
  359.7 3.0 collective-permute-done.60
  364.6 3.3 multiply_convert_fusion.3
  377.1 5.2 %collective-permute-done.62 = bf16[64,1024]{1,0:T(8,128)(2,1)S(1)} collective-permute-done((bf16[64,1024]{1,0:T(8,128)(2,1)}, bf16[64,1024]{1,0:T(8,128)(2,1)S(1)}, u32[]{:S(2)}, u32[]{:S(2)}) %collective-permute-start.62) | collective-permute-done | bytes 131104 | tf_op jit(solution)/shard_map/ppermute | solution.py:37
  384.6 3.7 collective-permute-start.68
  390.3 3.1 collective-permute-start.66
  408.2 6.0 %collective-permute-done.84 = bf16[1024,128]{1,0:T(8,128)(2,1)S(1)} collective-permute-done((bf16[1024,128]{1,0:T(8,128)(2,1)S(1)}, bf16[1024,128]{1,0:T(8,128)(2,1)S(1)}, u32[]{:S(2)}, u32[]{:S(2)}) %collective-permute-start.84) | collective-permute-done | bytes 262176 | tf_op jit(solution)/shard_map/ppermute | solution.py:55
  415.6 4.2 collective-permute-done.83
  421.8 3.7 collective-permute-done.80
  425.5 5.1 %collective-permute-done.79 = bf16[1024,128]{1,0:T(8,128)(2,1)S(1)} collective-permute-done((bf16[1024,128]{1,0:T(8,128)(2,1)S(1)}, bf16[1024,128]{1,0:T(8,128)(2,1)S(1)}, u32[]{:S(2)}, u32[]{:S(2)}) %collective-permute-start.79) | collective-permute-done | bytes 262176 | tf_op jit(solution)/shard_map/ppermute | solution.py:55
  441.1 8.5 %collective-permute-done.76 = bf16[128,2048]{1,0:T(8,128)(2,1)S(1)} collective-permute-done((bf16[128,2048]{1,0:T(8,128)(2,1)S(1)}, bf16[128,2048]{1,0:T(8,128)(2,1)S(1)}, u32[]{:S(2)}, u32[]{:S(2)}) %collective-permute-start.76) | collective-permute-done | bytes 524320 | tf_op jit(solution)/shard_map/ppermute | solution.py:55
  450.6 10.3 %collective-permute-done.75 = bf16[128,2048]{1,0:T(8,128)(2,1)S(1)} collective-permute-done((bf16[128,2048]{1,0:T(8,128)(2,1)S(1)}, bf16[128,2048]{1,0:T(8,128)(2,1)S(1)}, u32[]{:S(2)}, u32[]{:S(2)}) %collective-permute-start.75) | collective-permute-done | bytes 524320 | tf_op jit(solution)/shard_map/ppermute | solution.py:55
  461.2 10.9 %collective-permute-done.72 = bf16[128,2048]{1,0:T(8,128)(2,1)S(1)} collective-permute-done((bf16[128,2048]{1,0:T(8,128)(2,1)S(1)}, bf16[128,2048]{1,0:T(8,128)(2,1)S(1)}, u32[]{:S(2)}, u32[]{:S(2)}) %collective-permute-start.72) | collective-permute-done | bytes 524320 | tf_op jit(solution)/shard_map/ppermute | solution.py:55
  472.1 10.2 %collective-permute-done.71 = bf16[128,2048]{1,0:T(8,128)(2,1)S(1)} collective-permute-done((bf16[128,2048]{1,0:T(8,128)(2,1)S(1)}, bf16[128,2048]{1,0:T(8,128)(2,1)S(1)}, u32[]{:S(2)}, u32[]{:S(2)}) %collective-permute-start.71) | collective-permute-done | bytes 524320 | tf_op jit(solution)/shard_map/ppermute | solution.py:55
  485.0 3.9 stack.87
  496.1 4.4 collective-permute-start.106
  501.8 3.2 collective-permute-done.105
  (567 shorter events, 214.6 us)
Async XLA Ops:
  3.3 27.3 %collective-permute-start.8 = (bf16[256,1368]{0,1:T(8,128)(2,1)}, bf16[256,1368]{0,1:T(8,128)(2,1)}, u32[]{:S(2)}, u32[]{:S(2)}) collective-permute-start(bf16[256,1368]{0,1:T(8,128)(2,1)} %get-tuple-element.45), channel_id=1, source_target_pairs={{0,16},{16,0},{1,17},{17,1},{2,18},{18,2},{3,19},{19,3},{4,20},{20... | collective-permute-start | bytes 2101256 | tf_op jit(solution)/shard_map/ppermute | solution.py:32
  6.3 27.1 %collective-permute-start.7 = (bf16[256,1368]{0,1:T(8,128)(2,1)}, bf16[256,1368]{0,1:T(8,128)(2,1)}, u32[]{:S(2)}, u32[]{:S(2)}) collective-permute-start(bf16[256,1368]{0,1:T(8,128)(2,1)} %get-tuple-element.45), channel_id=1, source_target_pairs={{0,8},{8,0},{1,9},{9,1},{2,10},{10,2},{3,11},{11,3},{4,12},{12,4},... | collective-permute-start | bytes 2101256 | tf_op jit(solution)/shard_map/ppermute | solution.py:32
  9.0 28.6 %collective-permute-start.3 = (bf16[256,1368]{0,1:T(8,128)(2,1)}, bf16[256,1368]{0,1:T(8,128)(2,1)}, u32[]{:S(2)}, u32[]{:S(2)}) collective-permute-start(bf16[256,1368]{0,1:T(8,128)(2,1)} %get-tuple-element.43), channel_id=1, source_target_pairs={{0,16},{16,0},{1,17},{17,1},{2,18},{18,2},{3,19},{19,3},{4,20},{20... | collective-permute-start | bytes 2101256 | tf_op jit(solution)/shard_map/ppermute | solution.py:32
  9.5 32.4 %collective-permute-start.2 = (bf16[256,1368]{0,1:T(8,128)(2,1)}, bf16[256,1368]{0,1:T(8,128)(2,1)}, u32[]{:S(2)}, u32[]{:S(2)}) collective-permute-start(bf16[256,1368]{0,1:T(8,128)(2,1)} %get-tuple-element.43), channel_id=1, source_target_pairs={{0,8},{8,0},{1,9},{9,1},{2,10},{10,2},{3,11},{11,3},{4,12},{12,4},... | collective-permute-start | bytes 2101256 | tf_op jit(solution)/shard_map/ppermute | solution.py:32
  25.4 38.7 %collective-permute-start.46 = (bf16[64,1024]{1,0:T(8,128)(2,1)}, bf16[64,1024]{1,0:T(8,128)(2,1)S(1)}, u32[]{:S(2)}, u32[]{:S(2)}) collective-permute-start(bf16[64,1024]{1,0:T(8,128)(2,1)} %get-tuple-element.124), channel_id=1, source_target_pairs={{0,3},{1,0},{2,1},{3,2},{4,7},{5,4},{6,5},{7,6},{8,11},{9,8},{10,9... | collective-permute-start | bytes 393224 | tf_op jit(solution)/shard_map/ppermute | solution.py:37
  30.6 33.5 %collective-permute-start.45 = (bf16[64,1024]{1,0:T(8,128)(2,1)}, bf16[64,1024]{1,0:T(8,128)(2,1)}, u32[]{:S(2)}, u32[]{:S(2)}) collective-permute-start(bf16[64,1024]{1,0:T(8,128)(2,1)} %get-tuple-element.125), channel_id=1, source_target_pairs={{0,2},{1,3},{2,0},{3,1},{4,6},{5,7},{6,4},{7,5},{8,10},{9,11},{10,... | collective-permute-start | bytes 393224 | tf_op jit(solution)/shard_map/ppermute | solution.py:37
  41.9 22.2 %collective-permute-start.44 = (bf16[64,1024]{1,0:T(8,128)(2,1)S(1)}, bf16[64,1024]{1,0:T(8,128)(2,1)}, u32[]{:S(2)}, u32[]{:S(2)}) collective-permute-start(bf16[64,1024]{1,0:T(8,128)(2,1)S(1)} %get-tuple-element.123), channel_id=1, source_target_pairs={{0,1},{1,2},{2,3},{3,0},{4,5},{5,6},{6,7},{7,4},{8,9},{9,10},{10,1... | collective-permute-start | bytes 393224 | tf_op jit(solution)/shard_map/ppermute | solution.py:37
  55.0 26.5 %collective-permute-start.11 = (f32[256,1368]{0,1:T(8,128)}, f32[256,1368]{0,1:T(8,128)}, u32[]{:S(2)}, u32[]{:S(2)}) collective-permute-start(f32[256,1368]{0,1:T(8,128)} %slice.727), channel_id=1, source_target_pairs={{0,4},{4,0},{1,5},{5,1},{2,6},{6,2},{3,7},{7,3},{8,12},{12,8},{9,1... | collective-permute-start | bytes 4202504 | tf_op jit(solution)/shard_map/ppermute | solution.py:41
  60.3 22.6 %collective-permute-start.6 = (f32[256,1368]{0,1:T(8,128)}, f32[256,1368]{0,1:T(8,128)}, u32[]{:S(2)}, u32[]{:S(2)}) collective-permute-start(f32[256,1368]{0,1:T(8,128)} %slice.723), channel_id=1, source_target_pairs={{0,4},{4,0},{1,5},{5,1},{2,6},{6,2},{3,7},{7,3},{8,12},{12,8},{9,1... | collective-permute-start | bytes 4202504 | tf_op jit(solution)/shard_map/ppermute | solution.py:41
  76.4 18.8 %collective-permute-start.14 = (bf16[1368,256]{1,0:T(8,128)(2,1)}, bf16[1368,256]{1,0:T(8,128)(2,1)S(1)}, u32[]{:S(2)}, u32[]{:S(2)}) collective-permute-start(bf16[1368,256]{1,0:T(8,128)(2,1)} %get-tuple-element.47), channel_id=1, source_target_pairs={{0,16},{16,0},{1,17},{17,1},{2,18},{18,2},{3,19},{19,3},{4,20},{20... | collective-permute-start | bytes 2101256 | tf_op jit(solution)/shard_map/ppermute | solution.py:32
  78.7 18.8 %collective-permute-start.13 = (bf16[1368,256]{1,0:T(8,128)(2,1)}, bf16[1368,256]{1,0:T(8,128)(2,1)S(1)}, u32[]{:S(2)}, u32[]{:S(2)}) collective-permute-start(bf16[1368,256]{1,0:T(8,128)(2,1)} %get-tuple-element.47), channel_id=1, source_target_pairs={{0,8},{8,0},{1,9},{9,1},{2,10},{10,2},{3,11},{11,3},{4,12},{12,4},... | collective-permute-start | bytes 2101256 | tf_op jit(solution)/shard_map/ppermute | solution.py:32
  80.0 43.4 %collective-permute-start = (bf16[64,1024]{0,1:T(8,128)(2,1)S(1)}, bf16[64,1024]{0,1:T(8,128)(2,1)S(1)}, u32[]{:S(2)}, u32[]{:S(2)}) collective-permute-start(bf16[64,1024]{0,1:T(8,128)(2,1)S(1)} %pad_maximum_fusion.17), channel_id=1, source_target_pairs={{0,4},{4,0},{1,5},{5,1},{2,6},{6,2},{3,7},{7,3},{8,12},{12,8},{9,1... | collective-permute-start | bytes 393224 | tf_op jit(solution)/shard_map/ppermute | solution.py:41
  81.5 62.6 %collective-permute-start.31 = (bf16[256,1368]{0,1:T(8,128)(2,1)}, bf16[256,1368]{0,1:T(8,128)(2,1)S(1)}, u32[]{:S(2)}, u32[]{:S(2)}) collective-permute-start(bf16[256,1368]{0,1:T(8,128)(2,1)} %get-tuple-element.44), channel_id=1, source_target_pairs={{0,16},{16,0},{1,17},{17,1},{2,18},{18,2},{3,19},{19,3},{4,20},{20... | collective-permute-start | bytes 2101256 | tf_op jit(solution)/shard_map/ppermute | solution.py:32
  97.5 18.9 %collective-permute-start.15 = (bf16[1368,128]{1,0:T(8,128)(2,1)S(1)}, bf16[1368,128]{1,0:T(8,128)(2,1)S(1)}, u32[]{:S(2)}, u32[]{:S(2)}) collective-permute-start(bf16[1368,128]{1,0:T(8,128)(2,1)S(1)} %slice.728), channel_id=1, source_target_pairs={{0,16},{16,0},{1,17},{17,1},{2,18},{18,2},{3,19},{19,3},{4,20},{20... | collective-permute-start | bytes 1050632 | tf_op jit(solution)/shard_map/ppermute | solution.py:32
  118.4 22.8 %collective-permute-start.18 = (bf16[128,1024]{0,1:T(8,128)(2,1)S(1)}, bf16[128,1024]{0,1:T(8,128)(2,1)S(1)}, u32[]{:S(2)}, u32[]{:S(2)}) collective-permute-start(bf16[128,1024]{0,1:T(8,128)(2,1)S(1)} %pad_maximum_fusion.19), channel_id=1, source_target_pairs={{0,2},{1,3},{2,0},{3,1},{4,6},{5,7},{6,4},{7,5},{8,10},{9,11},{10,... | collective-permute-start | bytes 786440 | tf_op jit(solution)/shard_map/ppermute | solution.py:37
  120.5 20.8 %collective-permute-start.17 = (bf16[128,1024]{0,1:T(8,128)(2,1)S(1)}, bf16[128,1024]{0,1:T(8,128)(2,1)S(1)}, u32[]{:S(2)}, u32[]{:S(2)}) collective-permute-start(bf16[128,1024]{0,1:T(8,128)(2,1)S(1)} %pad_maximum_fusion.18), channel_id=1, source_target_pairs={{0,1},{1,2},{2,3},{3,0},{4,5},{5,6},{6,7},{7,4},{8,9},{9,10},{10,1... | collective-permute-start | bytes 786440 | tf_op jit(solution)/shard_map/ppermute | solution.py:37
  123.7 24.3 %collective-permute-start.30 = (bf16[256,1368]{0,1:T(8,128)(2,1)S(1)}, bf16[256,1368]{0,1:T(8,128)(2,1)S(1)}, u32[]{:S(2)}, u32[]{:S(2)}) collective-permute-start(bf16[256,1368]{0,1:T(8,128)(2,1)S(1)} %copy-done.28), channel_id=1, source_target_pairs={{0,8},{8,0},{1,9},{9,1},{2,10},{10,2},{3,11},{11,3},{4,12},{12,4},... | collective-permute-start | bytes 2101256 | tf_op jit(solution)/shard_map/ppermute | solution.py:32
  126.3 22.8 %collective-permute-start.26 = (bf16[256,1368]{0,1:T(8,128)(2,1)S(1)}, bf16[256,1368]{0,1:T(8,128)(2,1)S(1)}, u32[]{:S(2)}, u32[]{:S(2)}) collective-permute-start(bf16[256,1368]{0,1:T(8,128)(2,1)S(1)} %copy-done.27), channel_id=1, source_target_pairs={{0,16},{16,0},{1,17},{17,1},{2,18},{18,2},{3,19},{19,3},{4,20},{20... | collective-permute-start | bytes 2101256 | tf_op jit(solution)/shard_map/ppermute | solution.py:32
  144.1 57.9 %collective-permute-start.52 = (bf16[64,1024]{1,0:T(8,128)(2,1)}, bf16[64,1024]{1,0:T(8,128)(2,1)}, u32[]{:S(2)}, u32[]{:S(2)}) collective-permute-start(bf16[64,1024]{1,0:T(8,128)(2,1)} %get-tuple-element.121), channel_id=1, source_target_pairs={{0,3},{1,0},{2,1},{3,2},{4,7},{5,4},{6,5},{7,6},{8,11},{9,8},{10,9... | collective-permute-start | bytes 393224 | tf_op jit(solution)/shard_map/ppermute | solution.py:37
  148.0 53.9 %collective-permute-start.51 = (bf16[64,1024]{1,0:T(8,128)(2,1)}, bf16[64,1024]{1,0:T(8,128)(2,1)}, u32[]{:S(2)}, u32[]{:S(2)}) collective-permute-start(bf16[64,1024]{1,0:T(8,128)(2,1)} %get-tuple-element.122), channel_id=1, source_target_pairs={{0,2},{1,3},{2,0},{3,1},{4,6},{5,7},{6,4},{7,5},{8,10},{9,11},{10,... | collective-permute-start | bytes 393224 | tf_op jit(solution)/shard_map/ppermute | solution.py:37
  149.2 52.8 %collective-permute-start.50 = (bf16[64,1024]{1,0:T(8,128)(2,1)S(1)}, bf16[64,1024]{1,0:T(8,128)(2,1)}, u32[]{:S(2)}, u32[]{:S(2)}) collective-permute-start(bf16[64,1024]{1,0:T(8,128)(2,1)S(1)} %get-tuple-element.120), channel_id=1, source_target_pairs={{0,1},{1,2},{2,3},{3,0},{4,5},{5,6},{6,7},{7,4},{8,9},{9,10},{10,1... | collective-permute-start | bytes 393224 | tf_op jit(solution)/shard_map/ppermute | solution.py:37
  156.5 23.3 %collective-permute-start.23 = (bf16[128,1024]{0,1:T(8,128)(2,1)S(1)}, bf16[128,1024]{0,1:T(8,128)(2,1)S(1)}, u32[]{:S(2)}, u32[]{:S(2)}) collective-permute-start(bf16[128,1024]{0,1:T(8,128)(2,1)S(1)} %fusion.131), channel_id=1, source_target_pairs={{0,2},{1,3},{2,0},{3,1},{4,6},{5,7},{6,4},{7,5},{8,10},{9,11},{10,... | collective-permute-start | bytes 786440 | tf_op jit(solution)/shard_map/ppermute | solution.py:32
  157.4 24.3 %collective-permute-start.24 = (bf16[128,1024]{0,1:T(8,128)(2,1)S(1)}, bf16[128,1024]{0,1:T(8,128)(2,1)S(1)}, u32[]{:S(2)}, u32[]{:S(2)}) collective-permute-start(bf16[128,1024]{0,1:T(8,128)(2,1)S(1)} %fusion.131), channel_id=1, source_target_pairs={{0,1},{1,2},{2,3},{3,0},{4,5},{5,6},{6,7},{7,4},{8,9},{9,10},{10,1... | collective-permute-start | bytes 786440 | tf_op jit(solution)/shard_map/ppermute | solution.py:32
  198.7 18.7 %collective-permute-start.34 = (f32[256,1368]{0,1:T(8,128)S(1)}, f32[256,1368]{0,1:T(8,128)S(1)}, u32[]{:S(2)}, u32[]{:S(2)}) collective-permute-start(f32[256,1368]{0,1:T(8,128)S(1)} %slice.767), channel_id=1, source_target_pairs={{0,4},{4,0},{1,5},{5,1},{2,6},{6,2},{3,7},{7,3},{8,12},{12,8},{9,1... | collective-permute-start | bytes 4202504 | tf_op jit(solution)/shard_map/ppermute | solution.py:41
  200.7 17.2 %collective-permute-start.29 = (f32[256,1368]{0,1:T(8,128)S(1)}, f32[256,1368]{0,1:T(8,128)S(1)}, u32[]{:S(2)}, u32[]{:S(2)}) collective-permute-start(f32[256,1368]{0,1:T(8,128)S(1)} %slice.763), channel_id=1, source_target_pairs={{0,4},{4,0},{1,5},{5,1},{2,6},{6,2},{3,7},{7,3},{8,12},{12,8},{9,1... | collective-permute-start | bytes 4202504 | tf_op jit(solution)/shard_map/ppermute | solution.py:41
  211.5 15.3 %collective-permute-start.37 = (bf16[1368,256]{1,0:T(8,128)(2,1)S(1)}, bf16[1368,256]{1,0:T(8,128)(2,1)S(1)}, u32[]{:S(2)}, u32[]{:S(2)}) collective-permute-start(bf16[1368,256]{1,0:T(8,128)(2,1)S(1)} %copy-done.29), channel_id=1, source_target_pairs={{0,16},{16,0},{1,17},{17,1},{2,18},{18,2},{3,19},{19,3},{4,20},{20... | collective-permute-start | bytes 2101256 | tf_op jit(solution)/shard_map/ppermute | solution.py:32
  215.9 16.2 %collective-permute-start.36 = (bf16[1368,256]{1,0:T(8,128)(2,1)S(1)}, bf16[1368,256]{1,0:T(8,128)(2,1)S(1)}, u32[]{:S(2)}, u32[]{:S(2)}) collective-permute-start(bf16[1368,256]{1,0:T(8,128)(2,1)S(1)} %copy-done.29), channel_id=1, source_target_pairs={{0,8},{8,0},{1,9},{9,1},{2,10},{10,2},{3,11},{11,3},{4,12},{12,4},... | collective-permute-start | bytes 2101256 | tf_op jit(solution)/shard_map/ppermute | solution.py:32
  217.3 14.8 %collective-permute-start.85 = (bf16[256,1024]{1,0:T(8,128)(2,1)S(1)}, bf16[256,1024]{1,0:T(8,128)(2,1)S(1)}, u32[]{:S(2)}, u32[]{:S(2)}) collective-permute-start(bf16[256,1024]{1,0:T(8,128)(2,1)S(1)} %get-tuple-element.21), channel_id=1, source_target_pairs={{0,4},{4,0},{1,5},{5,1},{2,6},{6,2},{3,7},{7,3},{8,12},{12,8},{9,1... | collective-permute-start | bytes 1572872 | tf_op jit(solution)/shard_map/ppermute | solution.py:41
  217.4 17.4 %collective-permute-start.89 = (bf16[256,1024]{1,0:T(8,128)(2,1)S(1)}, bf16[256,1024]{1,0:T(8,128)(2,1)S(1)}, u32[]{:S(2)}, u32[]{:S(2)}) collective-permute-start(bf16[256,1024]{1,0:T(8,128)(2,1)S(1)} %pad_maximum_fusion.16), channel_id=1, source_target_pairs={{0,4},{4,0},{1,5},{5,1},{2,6},{6,2},{3,7},{7,3},{8,12},{12,8},{9,1... | collective-permute-start | bytes 1572872 | tf_op jit(solution)/shard_map/ppermute | solution.py:41
  218.5 18.8 %collective-permute-start.35 = (bf16[256,1368]{0,1:T(8,128)(2,1)S(1)}, bf16[256,1368]{0,1:T(8,128)(2,1)S(1)}, u32[]{:S(2)}, u32[]{:S(2)}) collective-permute-start(bf16[256,1368]{0,1:T(8,128)(2,1)S(1)} %fusion.74), channel_id=1, source_target_pairs={{0,4},{4,0},{1,5},{5,1},{2,6},{6,2},{3,7},{7,3},{8,12},{12,8},{9,1... | collective-permute-start | bytes 2101256 | tf_op jit(solution)/shard_map/ppermute | solution.py:41
  226.8 58.9 %collective-permute-start.56 = (bf16[1024,256]{1,0:T(8,128)(2,1)S(1)}, bf16[1024,256]{1,0:T(8,128)(2,1)S(1)}, u32[]{:S(2)}, u32[]{:S(2)}) collective-permute-start(bf16[1024,256]{1,0:T(8,128)(2,1)S(1)} %copy-done.31), channel_id=1, source_target_pairs={{0,1},{1,2},{2,3},{3,0},{4,5},{5,6},{6,7},{7,4},{8,9},{9,10},{10,1... | collective-permute-start | bytes 1572872 | tf_op jit(solution)/shard_map/ppermute | solution.py:32
  232.1 53.6 %collective-permute-start.55 = (bf16[1024,256]{1,0:T(8,128)(2,1)S(1)}, bf16[1024,256]{1,0:T(8,128)(2,1)S(1)}, u32[]{:S(2)}, u32[]{:S(2)}) collective-permute-start(bf16[1024,256]{1,0:T(8,128)(2,1)S(1)} %copy-done.31), channel_id=1, source_target_pairs={{0,2},{1,3},{2,0},{3,1},{4,6},{5,7},{6,4},{7,5},{8,10},{9,11},{10,... | collective-permute-start | bytes 1572872 | tf_op jit(solution)/shard_map/ppermute | solution.py:32
  248.8 35.5 %collective-permute-start.41 = (bf16[128,1024]{0,1:T(8,128)(2,1)S(1)}, bf16[128,1024]{0,1:T(8,128)(2,1)S(1)}, u32[]{:S(2)}, u32[]{:S(2)}) collective-permute-start(bf16[128,1024]{0,1:T(8,128)(2,1)S(1)} %pad_maximum_fusion.24), channel_id=1, source_target_pairs={{0,2},{1,3},{2,0},{3,1},{4,6},{5,7},{6,4},{7,5},{8,10},{9,11},{10,... | collective-permute-start | bytes 786440 | tf_op jit(solution)/shard_map/ppermute | solution.py:37
  250.8 33.5 %collective-permute-start.40 = (bf16[128,1024]{0,1:T(8,128)(2,1)S(1)}, bf16[128,1024]{0,1:T(8,128)(2,1)S(1)}, u32[]{:S(2)}, u32[]{:S(2)}) collective-permute-start(bf16[128,1024]{0,1:T(8,128)(2,1)S(1)} %pad_maximum_fusion.23), channel_id=1, source_target_pairs={{0,1},{1,2},{2,3},{3,0},{4,5},{5,6},{6,7},{7,4},{8,9},{9,10},{10,1... | collective-permute-start | bytes 786440 | tf_op jit(solution)/shard_map/ppermute | solution.py:37
  255.8 39.6 %collective-permute-start.54 = (bf16[1024,256]{1,0:T(8,128)(2,1)S(1)}, bf16[1024,256]{1,0:T(8,128)(2,1)S(1)}, u32[]{:S(2)}, u32[]{:S(2)}) collective-permute-start(bf16[1024,256]{1,0:T(8,128)(2,1)S(1)} %copy-done.31), channel_id=1, source_target_pairs={{0,3},{1,0},{2,1},{3,2},{4,7},{5,4},{6,5},{7,6},{8,11},{9,8},{10,9... | collective-permute-start | bytes 1572872 | tf_op jit(solution)/shard_map/ppermute | solution.py:32
  298.8 48.6 %collective-permute-start.43 = (bf16[64,1024]{0,1:T(8,128)(2,1)S(1)}, bf16[64,1024]{0,1:T(8,128)(2,1)}, u32[]{:S(2)}, u32[]{:S(2)}) collective-permute-start(bf16[64,1024]{0,1:T(8,128)(2,1)S(1)} %pad_maximum_fusion.27), channel_id=1, source_target_pairs={{0,4},{4,0},{1,5},{5,1},{2,6},{6,2},{3,7},{7,3},{8,12},{12,8},{9,1... | collective-permute-start | bytes 393224 | tf_op jit(solution)/shard_map/ppermute | solution.py:41
  299.0 50.3 %collective-permute-start.20 = (bf16[64,1024]{0,1:T(8,128)(2,1)S(1)}, bf16[64,1024]{0,1:T(8,128)(2,1)}, u32[]{:S(2)}, u32[]{:S(2)}) collective-permute-start(bf16[64,1024]{0,1:T(8,128)(2,1)S(1)} %pad_maximum_fusion.22), channel_id=1, source_target_pairs={{0,4},{4,0},{1,5},{5,1},{2,6},{6,2},{3,7},{7,3},{8,12},{12,8},{9,1... | collective-permute-start | bytes 393224 | tf_op jit(solution)/shard_map/ppermute | solution.py:41
  300.5 55.2 %collective-permute-start.57 = (f32[64,1024]{1,0:T(8,128)S(1)}, f32[64,1024]{1,0:T(8,128)S(1)}, u32[]{:S(2)}, u32[]{:S(2)}) collective-permute-start(f32[64,1024]{1,0:T(8,128)S(1)} %slice.797), channel_id=1, source_target_pairs={{0,4},{4,0},{1,5},{5,1},{2,6},{6,2},{3,7},{7,3},{8,12},{12,8},{9,1... | collective-permute-start | bytes 786440 | tf_op jit(solution)/shard_map/ppermute | solution.py:41
  302.4 81.0 %collective-permute-start.65 = (f32[64,1024]{1,0:T(8,128)}, f32[64,1024]{1,0:T(8,128)}, u32[]{:S(2)}, u32[]{:S(2)}) collective-permute-start(f32[64,1024]{1,0:T(8,128)} %slice.803), channel_id=1, source_target_pairs={{0,4},{4,0},{1,5},{5,1},{2,6},{6,2},{3,7},{7,3},{8,12},{12,8},{9,1... | collective-permute-start | bytes 786440 | tf_op jit(solution)/shard_map/ppermute | solution.py:41
  359.6 15.1 %collective-permute-start.99 = (f32[128,256]{0,1:T(8,128)S(1)}, f32[128,256]{0,1:T(8,128)S(1)}, u32[]{:S(2)}, u32[]{:S(2)}) collective-permute-start(f32[128,256]{0,1:T(8,128)S(1)} %slice_select_fusion), channel_id=1, source_target_pairs={{0,4},{4,0},{1,5},{5,1},{2,6},{6,2},{3,7},{7,3},{8,12},{12,8},{9,1... | collective-permute-start | bytes 393224 | tf_op jit(solution)/shard_map/ppermute | solution.py:41
  395.0 37.5 %collective-permute-start.73 = (bf16[512,2048]{1,0:T(8,128)(2,1)S(1)}, bf16[512,2048]{1,0:T(8,128)(2,1)S(1)}, u32[]{:S(2)}, u32[]{:S(2)}) collective-permute-start(bf16[512,2048]{1,0:T(8,128)(2,1)S(1)} %slice.812), channel_id=1, source_target_pairs={{0,4},{4,0},{1,5},{5,1},{2,6},{6,2},{3,7},{7,3},{8,12},{12,8},{9,1... | collective-permute-start | bytes 6291464 | tf_op jit(solution)/shard_map/ppermute | solution.py:41
  403.3 34.0 %collective-permute-start.69 = (bf16[512,2048]{1,0:T(8,128)(2,1)S(1)}, bf16[512,2048]{1,0:T(8,128)(2,1)S(1)}, u32[]{:S(2)}, u32[]{:S(2)}) collective-permute-start(bf16[512,2048]{1,0:T(8,128)(2,1)S(1)} %slice.805), channel_id=1, source_target_pairs={{0,4},{4,0},{1,5},{5,1},{2,6},{6,2},{3,7},{7,3},{8,12},{12,8},{9,1... | collective-permute-start | bytes 6291464 | tf_op jit(solution)/shard_map/ppermute | solution.py:41
  433.8 15.8 %collective-permute-start.76 = (bf16[128,2048]{1,0:T(8,128)(2,1)S(1)}, bf16[128,2048]{1,0:T(8,128)(2,1)S(1)}, u32[]{:S(2)}, u32[]{:S(2)}) collective-permute-start(bf16[128,2048]{1,0:T(8,128)(2,1)S(1)} %get-tuple-element.38), channel_id=1, source_target_pairs={{0,24},{8,16},{16,8},{24,0},{1,25},{9,17},{17,9},{25,1},{2,26},{10... | collective-permute-start | bytes 1572872 | tf_op jit(solution)/shard_map/ppermute | solution.py:55
  435.2 25.7 %collective-permute-start.75 = (bf16[128,2048]{1,0:T(8,128)(2,1)S(1)}, bf16[128,2048]{1,0:T(8,128)(2,1)S(1)}, u32[]{:S(2)}, u32[]{:S(2)}) collective-permute-start(bf16[128,2048]{1,0:T(8,128)(2,1)S(1)} %get-tuple-element.39), channel_id=1, source_target_pairs={{0,16},{8,24},{16,0},{24,8},{1,17},{9,25},{17,1},{25,9},{2,18},{10... | collective-permute-start | bytes 1572872 | tf_op jit(solution)/shard_map/ppermute | solution.py:55
  436.3 24.6 %collective-permute-start.74 = (bf16[128,2048]{1,0:T(8,128)(2,1)S(1)}, bf16[128,2048]{1,0:T(8,128)(2,1)S(1)}, u32[]{:S(2)}, u32[]{:S(2)}) collective-permute-start(bf16[128,2048]{1,0:T(8,128)(2,1)S(1)} %get-tuple-element.37), channel_id=1, source_target_pairs={{0,8},{8,0},{16,24},{24,16},{1,9},{9,1},{17,25},{25,17},{2,10},{10... | collective-permute-start | bytes 1572872 | tf_op jit(solution)/shard_map/ppermute | solution.py:55
  438.6 33.5 %collective-permute-start.72 = (bf16[128,2048]{1,0:T(8,128)(2,1)S(1)}, bf16[128,2048]{1,0:T(8,128)(2,1)S(1)}, u32[]{:S(2)}, u32[]{:S(2)}) collective-permute-start(bf16[128,2048]{1,0:T(8,128)(2,1)S(1)} %get-tuple-element.33), channel_id=1, source_target_pairs={{0,24},{8,16},{16,8},{24,0},{1,25},{9,17},{17,9},{25,1},{2,26},{10... | collective-permute-start | bytes 1572872 | tf_op jit(solution)/shard_map/ppermute | solution.py:55
  440.0 42.3 %collective-permute-start.71 = (bf16[128,2048]{1,0:T(8,128)(2,1)S(1)}, bf16[128,2048]{1,0:T(8,128)(2,1)S(1)}, u32[]{:S(2)}, u32[]{:S(2)}) collective-permute-start(bf16[128,2048]{1,0:T(8,128)(2,1)S(1)} %get-tuple-element.34), channel_id=1, source_target_pairs={{0,16},{8,24},{16,0},{24,8},{1,17},{9,25},{17,1},{25,9},{2,18},{10... | collective-permute-start | bytes 1572872 | tf_op jit(solution)/shard_map/ppermute | solution.py:55
  449.6 32.8 %collective-permute-start.70 = (bf16[128,2048]{1,0:T(8,128)(2,1)S(1)}, bf16[128,2048]{1,0:T(8,128)(2,1)S(1)}, u32[]{:S(2)}, u32[]{:S(2)}) collective-permute-start(bf16[128,2048]{1,0:T(8,128)(2,1)S(1)} %get-tuple-element.32), channel_id=1, source_target_pairs={{0,8},{8,0},{16,24},{24,16},{1,9},{9,1},{17,25},{25,17},{2,10},{10... | collective-permute-start | bytes 1572872 | tf_op jit(solution)/shard_map/ppermute | solution.py:55
  (140 other events, 1373.8 us)
